TPU v7x, 32 devices: a whole 2x2x4 slice. The times are simulated.
32 devices in a mesh: dp: 2 (over x), tp: 4 (over z), ep: 4 (over y, core).
Axes of the slice: x: 2, y: 2, z: 4, core: 2. Of those that a mesh axis runs over, the one named last changes fastest.
Arguments:
- x: bfloat16 [2048, 2048], P(('dp', 'tp', 'ep')), parts along dimension 0
- route_idx: int32 [2048, 8], P(('dp', 'tp', 'ep')), parts along dimension 0
- gates: float32 [2048, 8], P(('dp', 'tp', 'ep')), parts along dimension 0
- w1: bfloat16 [64, 2048, 1024], P('ep', None, 'tp')
- w3: bfloat16 [64, 2048, 1024], P('ep', None, 'tp')
- w2: bfloat16 [64, 1024, 2048], P('ep', 'tp')
Outputs:
- output: bfloat16 [2048, 2048], P(('dp', 'tp', 'ep')), parts along dimension 0
There are 2 independent parts. A program takes and returns all parts, laid end to end along the dimension named above; an argument that names none is the same for every part.
All inputs are finite; a program needn't handle non-finite values.
Results may differ from a plain program's by a relative error of at most 0.00782163.
Values are sent between devices in bfloat16 or wider.
A program may use at most 1 GiB of HBM per device.

v0:
```python
import functools

import jax
import jax.numpy as jnp
from jax import lax
from jax.experimental import pallas as pl
from jax.experimental.pallas import tpu as pltpu
from jax.sharding import PartitionSpec as P

TM = 128
BR = 16
LAG = 3
NS = 8
NO = NS + 1
TC = 128
SIZES = (704, 832, 960, 1024, 1088, 1152, 1216, 1280, 1344, 1408, 1472, 1600, 1792, 2304)
MESH = pl.DeviceIdType.MESH


def expert_kernel(meta, dest, x, w1, w3, w2, out, obuf, carry, cnt, sem):
    e = pl.program_id(0)
    n_tok = x.shape[0]
    n_blk = TM // 8

    def copy(src, half, to, slot):
        return pltpu.make_async_copy(src, out.at[half, pl.ds(pl.multiple_of(to * 8, 8), 8)], sem.at[slot])

    def drain(slot):
        def one(_, c):
            copy(obuf.at[slot, pl.ds(0, 8)], 0, 0, slot).wait()
            return c
        lax.fori_loop(0, cnt[slot], one, 0)

    @pl.when(e == 0)
    def _():
        cnt[0] = 0
        cnt[1] = 0
        cnt[2] = 0
        carry[...] = jnp.zeros_like(carry)

    begin = (0, meta[e, 0])
    stop = (meta[e, 0], meta[e, 0] + meta[e, 1])
    place = (meta[e, 2], meta[e, 3])
    short = (meta[e, 4] > 0, meta[e, 5] > 0)
    blocks = stop[1]

    def tile(i, c):
        rows = lax.broadcasted_iota(jnp.int32, (TM, n_tok), 0) + i * TM
        pick = jnp.where(dest[0] == rows, 1.0, 0.0).astype(jnp.bfloat16)
        xs = jnp.dot(pick, x[...], preferred_element_type=jnp.float32).astype(jnp.bfloat16)
        a = jnp.dot(xs, w1[0], preferred_element_type=jnp.float32)
        b = jnp.dot(xs, w3[0], preferred_element_type=jnp.float32)
        h = (jax.nn.silu(a) * b).astype(jnp.bfloat16)
        slot = cnt[2]
        drain(slot)
        obuf[slot] = jnp.dot(h, w2[0], preferred_element_type=jnp.float32)
        low = i * n_blk
        n = jnp.minimum(n_blk, blocks - low)
        kept = jnp.int32(0)
        for half in (0, 1):
            some = stop[half] > begin[half]
            first = begin[half] - low
            final = stop[half] - 1 - low

            @pl.when(jnp.logical_and(some, jnp.logical_and(first >= 0, first < n_blk)))
            def _(half=half, first=first):
                at = pl.ds(pl.multiple_of(first * 8, 8), 8)
                obuf[slot, at] += carry[half]
                carry[half] = jnp.zeros_like(carry[half])

            keep = jnp.logical_and(jnp.logical_and(some, short[half]), jnp.logical_and(final >= 0, final < n_blk))

            @pl.when(keep)
            def _(half=half, final=final):
                carry[half] = obuf[slot, pl.ds(pl.multiple_of(final * 8, 8), 8)]
            kept = kept + jnp.where(keep, 1, 0)

        def put(k, c):
            g = low + k
            late = g >= begin[1]
            half = jnp.where(late, 1, 0)
            to = jnp.where(late, place[1] + g - begin[1], place[0] + g)
            held = jnp.where(late, jnp.logical_and(short[1], g == stop[1] - 1).astype(jnp.int32),
                             jnp.logical_and(short[0], g == stop[0] - 1).astype(jnp.int32))

            @pl.when(held == 0)
            def _():
                copy(obuf.at[slot, pl.ds(pl.multiple_of(k * 8, 8), 8)], half, to, slot).start()
            return c

        lax.fori_loop(0, n, put, 0)
        cnt[slot] = n - kept
        cnt[2] = 1 - slot
        return c

    lax.fori_loop(0, (blocks + n_blk - 1) // n_blk, tile, 0)

    @pl.when(e == pl.num_programs(0) - 1)
    def _():
        drain(0)
        drain(1)
        for half in (0, 1):
            @pl.when(meta[e, 6 + half] >= 0)
            def _(half=half):
                last = copy(carry.at[half], half, meta[e, 6 + half], 0)
                last.start()
                last.wait()


def chain_kernel(n, blocks, count, rows, gates, src, out, own, rbuf, sbuf, obuf, own_sem, send_sem, recv_sem, credit):
    z = lax.axis_index('tp')
    barrier = pltpu.get_barrier_semaphore()

    @pl.when(z > 0)
    def _():
        pl.semaphore_signal(barrier, inc=1, device_id={'tp': z - 1}, device_id_type=MESH)

    @pl.when(z < n - 1)
    def _():
        pl.semaphore_signal(barrier, inc=1, device_id={'tp': z + 1}, device_id_type=MESH)

    pl.semaphore_wait(barrier, jnp.where(z > 0, 1, 0) + jnp.where(z < n - 1, 1, 0))

    def load(d, k):
        s = lax.rem(k, NO)
        return pltpu.make_async_copy(src.at[1 - d, pl.ds(pl.multiple_of(k * BR, BR), BR)], own.at[d, s], own_sem.at[d, s])

    def send(d, k, buf, s_buf):
        s = lax.rem(k, NS)
        to = z + 1 if d == 0 else z - 1
        return pltpu.make_async_remote_copy(
            src_ref=buf.at[d, s_buf], dst_ref=rbuf.at[d, s], send_sem=send_sem.at[d, s], recv_sem=recv_sem.at[d, s],
            device_id={'tp': to}, device_id_type=MESH)

    per = TC // BR

    def gated(j):
        col = lax.broadcasted_iota(jnp.int32, (rows.shape[0], TC), 1) + j * TC
        g = jnp.zeros((rows.shape[0], TC), jnp.float32)
        for k in range(rows.shape[1]):
            g = g + jnp.where(rows[:, k:k + 1] == col, gates[:, k:k + 1], 0.0)
        g1 = g.astype(jnp.bfloat16)
        rest = g - g1.astype(jnp.float32)
        g2 = rest.astype(jnp.bfloat16)
        g3 = (rest - g2.astype(jnp.float32)).astype(jnp.bfloat16)
        g = jnp.concatenate([g1, g2, g3], axis=1)
        wide = min(256, out.shape[1])
        row = lax.broadcasted_iota(jnp.int32, (TC, wide), 0) + j * TC

        def columns(q, c):
            at = pl.ds(pl.multiple_of(q * wide, wide), wide)
            o = jnp.where(row < count[0], obuf[:, at].astype(jnp.float32), 0.0).astype(jnp.bfloat16)
            out[:, at] += jnp.dot(g, jnp.concatenate([o, o, o], axis=0), preferred_element_type=jnp.float32)
            return c

        lax.fori_loop(0, out.shape[1] // wide, columns, 0)

    def step(i, c):
        work = []
        for d in (0, 1):
            p = z if d == 0 else n - 1 - z
            k = i - LAG * p
            work.append((d, p, k, jnp.logical_and(k >= 0, k < blocks)))

        for d, p, k, live in work:
            @pl.when(live)
            def _(d=d, p=p, k=k):
                @pl.when(jnp.logical_and(p < n - 1, k >= NS))
                def _():
                    send(d, k - NS, sbuf, lax.rem(k, NS)).wait_send()

                @pl.when(k == 0)
                def _():
                    load(d, k).start()

                @pl.when(k + 1 < blocks)
                def _():
                    load(d, k + 1).start()

                load(d, k).wait()

        for d, p, k, live in work:
            @pl.when(jnp.logical_and(live, p == 0))
            def _(d=d, k=k):
                @pl.when(k >= NS)
                def _():
                    pl.semaphore_wait(credit.at[d], 1)
                send(d, k, own, lax.rem(k, NO)).start()

        for d, p, k, live in work:
            @pl.when(jnp.logical_and(live, p > 0))
            def _(d=d, p=p, k=k):
                s = lax.rem(k, NS)
                send(d, k, sbuf, s).wait_recv()

                @pl.when(p < n - 1)
                def _():
                    sbuf[d, s] = rbuf[d, s] + own[d, lax.rem(k, NO)]

                @pl.when(p == n - 1)
                def _():
                    to = pl.multiple_of(lax.rem(k, per) * BR, BR)
                    obuf[pl.ds(to, BR)] = (rbuf[d, s] + own[d, lax.rem(k, NO)]).astype(jnp.bfloat16)

                @pl.when(k + NS < blocks)
                def _():
                    back = z - 1 if d == 0 else z + 1
                    pl.semaphore_signal(credit.at[d], inc=1, device_id={'tp': back}, device_id_type=MESH)

        for d, p, k, live in work:
            @pl.when(jnp.logical_and(live, jnp.logical_and(p > 0, p < n - 1)))
            def _(d=d, k=k):
                @pl.when(k >= NS)
                def _():
                    pl.semaphore_wait(credit.at[d], 1)
                send(d, k, sbuf, lax.rem(k, NS)).start()

        k = i - LAG * (n - 1)

        @pl.when(jnp.logical_and(jnp.logical_or(z == 0, z == n - 1), jnp.logical_and(k >= 0, jnp.logical_or(lax.rem(k + per, per) == per - 1, k == blocks - 1))))
        def _():
            gated(k // per)
        return c

    @pl.when(jnp.logical_or(z == 0, z == n - 1))
    def _():
        out[...] = jnp.zeros_like(out)

    lax.fori_loop(0, blocks + LAG * (n - 1), step, 0)

    for d in (0, 1):
        p = z if d == 0 else n - 1 - z

        @pl.when(p < n - 1)
        def _(d=d):
            for k in range(blocks - NS, blocks):
                send(d, k, sbuf, k % NS).wait_send()


def gather_kernel(n, x, info, xout, iout, xbuf, ibuf, own_sem, xsend, isend, xrecv, irecv, out_sem):
    z = lax.axis_index('tp')
    j = lax.axis_index('ep')
    t_loc = x.shape[0]
    sib = j + 1 - 2 * lax.rem(j, 2)
    peer = lax.rem(j + 2, 4)
    blk = lambda zz, jj: zz * 4 + jj
    up, down = {'tp': z + 1}, {'tp': z - 1}
    me = blk(z, j)
    mine = (pltpu.make_async_copy(x, xbuf.at[me], own_sem.at[0]), pltpu.make_async_copy(info, ibuf.at[me], own_sem.at[1]))
    for m in mine:
        m.start()

    barrier = pltpu.get_barrier_semaphore()
    for other in (sib, peer):
        pl.semaphore_signal(barrier, inc=1, device_id={'ep': other}, device_id_type=MESH)

    @pl.when(z > 0)
    def _():
        pl.semaphore_signal(barrier, inc=1, device_id=down, device_id_type=MESH)

    @pl.when(z < n - 1)
    def _():
        pl.semaphore_signal(barrier, inc=1, device_id=up, device_id_type=MESH)

    pl.semaphore_wait(barrier, 2 + jnp.where(z > 0, 1, 0) + jnp.where(z < n - 1, 1, 0))

    def copies(b, i, dev):
        make = lambda buf, s, r: pltpu.make_async_remote_copy(
            src_ref=buf.at[b], dst_ref=buf.at[b], send_sem=s.at[i], recv_sem=r.at[b], device_id=dev, device_id_type=MESH)
        return make(ibuf, isend, irecv), make(xbuf, xsend, xrecv)

    def send(b, i, dev):
        for c in copies(b, i, dev):
            c.start()

    def sent(b, i, dev):
        for c in copies(b, i, dev):
            c.wait_send()

    def arrive(b):
        for c in copies(b, 0, {'ep': sib}):
            c.wait_recv()

    def keep(b):
        return pltpu.make_async_copy(xbuf.at[b], xout.at[pl.ds(pl.multiple_of(b * t_loc, t_loc), t_loc)], out_sem.at[b])

    def line(f):
        f(z, 0, True, True)
        for r in range(1, n):
            @pl.when(z >= r)
            def _(r=r):
                f(z - r, r, True, False)

            @pl.when(z + r < n)
            def _(r=r):
                f(z + r, r, False, True)

    def spread(act):
        def f(zz, r, ups, downs):
            b = blk(zz, j)
            if act is send:
                if r == 0:
                    for m in mine:
                        m.wait()
                else:
                    arrive(b)
            if ups:
                @pl.when(z < n - 1)
                def _():
                    act(b, r, up)
            if downs:
                @pl.when(z > 0)
                def _():
                    act(b, n + r, down)
            act(b, 2 * n + zz, {'ep': peer})
            act(b, 3 * n + zz, {'ep': sib})
            if act is send:
                keep(b).start()
        return f

    def relay(act):
        def f(zz, r, ups, downs):
            b = blk(zz, peer)
            if act is send:
                arrive(b)
            act(b, 4 * n + zz, {'ep': sib})
            if act is send:
                keep(b).start()
        return f

    line(spread(send))
    line(relay(send))
    for other in (sib, lax.rem(sib + 2, 4)):
        def take(zz, r, ups, downs, other=other):
            arrive(blk(zz, other))
            keep(blk(zz, other)).start()
        line(take)
    every = pltpu.make_async_copy(ibuf, iout, own_sem.at[0])
    every.start()
    line(spread(sent))
    line(relay(sent))
    for b in range(4 * n):
        keep(b).wait()
    every.wait()


def finish_kernel(n, py, out, ra, sb, rb, yb, rc, a_send, a_recv, b_send, b_recv, c_send, c_recv):
    z = lax.axis_index('tp')
    j = lax.axis_index('ep')
    t_loc = out.shape[0]
    ln = t_loc // 2
    y, c = j // 2, lax.rem(j, 2)
    sib = j + 1 - 2 * c
    peer = lax.rem(j + 2, 4)
    end = jnp.logical_or(z == 0, z == n - 1)
    low = z < n // 2
    across = jnp.where(z == 0, 1, jnp.where(z == 1, 0, jnp.where(z == n - 1, n - 2, n - 1)))
    barrier = pltpu.get_barrier_semaphore()
    pl.semaphore_signal(barrier, inc=1, device_id={'tp': across}, device_id_type=MESH)

    @pl.when(end)
    def _():
        for other in (sib, peer):
            pl.semaphore_signal(barrier, inc=1, device_id={'ep': other}, device_id_type=MESH)

    pl.semaphore_wait(barrier, jnp.where(end, 3, 1))

    inner = jnp.where(low, 1, 0)
    starts = [pl.multiple_of((inner if q < 2 else 1 - inner) * t_loc + (q % 2) * ln, ln) for q in range(4)]

    def to_sib(q, yy):
        at = pl.ds(starts[q], ln)
        return pltpu.make_async_remote_copy(
            src_ref=py.at[2 * yy + 1 - c, at], dst_ref=ra.at[yy, at], send_sem=a_send.at[q, yy], recv_sem=a_recv.at[q, yy],
            device_id={'ep': sib}, device_id_type=MESH)

    def to_peer(q):
        at = pl.ds(starts[q], ln)
        return pltpu.make_async_remote_copy(
            src_ref=sb.at[at], dst_ref=rb.at[at], send_sem=b_send.at[q], recv_sem=b_recv.at[q],
            device_id={'ep': peer}, device_id_type=MESH)

    def to_inner(q):
        return pltpu.make_async_remote_copy(
            src_ref=yb.at[q], dst_ref=rc.at[q], send_sem=c_send.at[q], recv_sem=c_recv.at[q],
            device_id={'tp': across}, device_id_type=MESH)

    @pl.when(end)
    def _():
        for q in range(4):
            to_sib(q, 1 - y).start()
        for q in range(4):
            to_sib(q, y).start()
        for q in range(4):
            at = pl.ds(starts[q], ln)
            to_sib(q, 1 - y).wait_recv()
            sb[at] = py[2 * (1 - y) + c, at] + ra[1 - y, at]
            to_peer(q).start()
        for q in range(4):
            at = pl.ds(starts[q], ln)
            to_sib(q, y).wait_recv()
            to_peer(q).wait_recv()
            v = ((py[2 * y + c, at] + ra[y, at]) + rb[at]).astype(jnp.bfloat16)
            if q < 2:
                yb[q] = v
                to_inner(q).start()
            else:
                out[pl.ds((q - 2) * ln, ln)] = v
        for q in range(4):
            to_sib(q, y).wait_send()
            to_sib(q, 1 - y).wait_send()
            to_peer(q).wait_send()
        for q in range(2):
            to_inner(q).wait_send()

    @pl.when(jnp.logical_not(end))
    def _():
        for q in range(2):
            to_inner(q).wait_recv()
            out[pl.ds(q * ln, ln)] = rc[q]


def solution(mesh):
    tp = mesh.shape['tp']
    ep = mesh.shape['ep']
    tok_spec = P(('dp', 'tp', 'ep'), None)

    def local(x, route_idx, gates, w1, w3, w2):
        t_loc, d = x.shape
        top = route_idx.shape[1]
        e_loc, _, f = w1.shape
        n_tok = t_loc * tp * ep
        n_half = n_tok // 2
        z = lax.axis_index('tp')
        j = lax.axis_index('ep')
        side = jnp.where(z >= tp // 2, 1, 0)

        own = jnp.concatenate([route_idx.astype(jnp.float32), gates], axis=1)
        ir = t_loc * 2 * top // 128
        any_ = pl.BlockSpec(memory_space=pl.ANY)
        vmem = pl.BlockSpec(memory_space=pltpu.VMEM)
        xa, info = pl.pallas_call(
            functools.partial(gather_kernel, tp),
            in_specs=[any_, any_],
            out_specs=[any_, any_],
            out_shape=[jax.ShapeDtypeStruct((n_tok, d), x.dtype), jax.ShapeDtypeStruct((tp * ep, ir, 128), jnp.float32)],
            scratch_shapes=[
                pltpu.VMEM((tp * ep, t_loc, d), x.dtype),
                pltpu.VMEM((tp * ep, ir, 128), jnp.float32),
                pltpu.SemaphoreType.DMA((2,)),
                pltpu.SemaphoreType.DMA((5 * tp,)),
                pltpu.SemaphoreType.DMA((5 * tp,)),
                pltpu.SemaphoreType.DMA((tp * ep,)),
                pltpu.SemaphoreType.DMA((tp * ep,)),
                pltpu.SemaphoreType.DMA((tp * ep,)),
            ],
            compiler_params=pltpu.CompilerParams(collective_id=20, has_side_effects=True),
            name='gather',
        )(x, own.reshape(ir, 128))
        info = info.reshape(n_tok, 2 * top)

        loc = info[:, :top].astype(jnp.int32) - j * e_loc
        ga = info[:, top:]
        ids = jnp.arange(e_loc, dtype=jnp.int32)
        hit = jnp.any(loc.T[None] == ids[:, None, None], axis=1)
        before = jnp.arange(n_half)[:, None] < jnp.arange(n_half)[None, :]
        hit2 = hit.reshape(e_loc * 2, n_half)
        pos = jnp.dot(hit2.astype(jnp.bfloat16), before.astype(jnp.bfloat16),
                      preferred_element_type=jnp.float32).astype(jnp.int32).reshape(e_loc, 2, n_half)
        n = jnp.sum(hit2.astype(jnp.int32), axis=1).reshape(e_loc, 2)
        off = jnp.sum(jnp.where(ids[:, None, None] > ids[None, :, None], n[None], 0), axis=1)
        total = jnp.sum(n, axis=0)
        lead = off % 8
        nb = jnp.where(n > 0, (lead + n + 7) // 8, 0)
        left = jnp.broadcast_to(jnp.where(total % 8 > 0, total // 8, -1)[None], (e_loc, 2))
        meta = jnp.concatenate([nb, off // 8, (off + n) % 8, left], axis=1)
        base = jnp.stack([lead[:, 0], nb[:, 0] * 8 + lead[:, 1]], axis=1)
        dest = jnp.where(hit, (base[:, :, None] + pos).reshape(e_loc, n_tok), -1)

        full = -(-n_half * top // TC) * TC
        part = pl.pallas_call(
            expert_kernel,
            grid_spec=pltpu.PrefetchScalarGridSpec(
                num_scalar_prefetch=1,
                grid=(e_loc,),
                in_specs=[
                    pl.BlockSpec((1, 1, n_tok), lambda e, m: (e, 0, 0)),
                    pl.BlockSpec((n_tok, d), lambda e, m: (0, 0)),
                    pl.BlockSpec((1, d, f), lambda e, m: (e, 0, 0)),
                    pl.BlockSpec((1, d, f), lambda e, m: (e, 0, 0)),
                    pl.BlockSpec((1, f, d), lambda e, m: (e, 0, 0)),
                ],
                out_specs=pl.BlockSpec(memory_space=pl.ANY),
                scratch_shapes=[
                    pltpu.VMEM((2, TM, d), jnp.float32),
                    pltpu.VMEM((2, 8, d), jnp.float32),
                    pltpu.SMEM((3,), jnp.int32),
                    pltpu.SemaphoreType.DMA((2,)),
                ]),
            out_shape=jax.ShapeDtypeStruct((2, full, d), jnp.float32),
            compiler_params=pltpu.CompilerParams(dimension_semantics=('arbitrary',), vmem_limit_bytes=60000 * 1024),
            name='experts',
        )(meta, dest.reshape(e_loc, 1, n_tok), xa, w1, w3, w2)

        row = (off[:, :, None] + pos)[:, side]
        mine = loc.reshape(2, n_half, top)[side]
        same = mine[:, :, None] == ids[None, None, :]
        rows = jnp.sum(jnp.where(same, row.T[:, None, :], 0), axis=2)
        rows = jnp.where(jnp.any(same, axis=2), rows, -1)
        order = lambda v: v.reshape(tp // 2, ep, t_loc, top).transpose(1, 0, 2, 3).reshape(n_half, top)

        def chain(size, ident):
            return pl.pallas_call(
                functools.partial(chain_kernel, tp, size // BR),
                in_specs=[pl.BlockSpec(memory_space=pltpu.SMEM), vmem, vmem, any_],
                out_specs=vmem,
                out_shape=jax.ShapeDtypeStruct((n_half, d), jnp.float32),
                scratch_shapes=[
                    pltpu.VMEM((2, NO, BR, d), jnp.float32),
                    pltpu.VMEM((2, NS, BR, d), jnp.float32),
                    pltpu.VMEM((2, NS, BR, d), jnp.float32),
                    pltpu.VMEM((TC, d), jnp.bfloat16),
                    pltpu.SemaphoreType.DMA((2, NO)),
                    pltpu.SemaphoreType.DMA((2, NS)),
                    pltpu.SemaphoreType.DMA((2, NS)),
                    pltpu.SemaphoreType.REGULAR((2,)),
                ],
                compiler_params=pltpu.CompilerParams(collective_id=ident, has_side_effects=True, vmem_limit_bytes=60000 * 1024),
                name=f'chain{size}',
            )

        sizes = tuple(s for s in SIZES if s < full) + (full,)
        need = jnp.max(total)
        which = jnp.sum((need > jnp.array(sizes[:-1], jnp.int32)).astype(jnp.int32))
        py = lax.switch(which, [chain(s, i + 1) for i, s in enumerate(sizes)],
                        total[side].reshape(1), order(rows), order(ga.reshape(2, n_half, top)[side]), part)

        return pl.pallas_call(
            functools.partial(finish_kernel, tp),
            in_specs=[vmem],
            out_specs=vmem,
            out_shape=jax.ShapeDtypeStruct((t_loc, d), x.dtype),
            scratch_shapes=[
                pltpu.VMEM((2, 2 * t_loc, d), jnp.float32),
                pltpu.VMEM((2 * t_loc, d), jnp.float32),
                pltpu.VMEM((2 * t_loc, d), jnp.float32),
                pltpu.VMEM((2, t_loc // 2, d), x.dtype),
                pltpu.VMEM((2, t_loc // 2, d), x.dtype),
                pltpu.SemaphoreType.DMA((4, 2)),
                pltpu.SemaphoreType.DMA((4, 2)),
                pltpu.SemaphoreType.DMA((4,)),
                pltpu.SemaphoreType.DMA((4,)),
                pltpu.SemaphoreType.DMA((2,)),
                pltpu.SemaphoreType.DMA((2,)),
            ],
            compiler_params=pltpu.CompilerParams(collective_id=21, has_side_effects=True, vmem_limit_bytes=60000 * 1024),
            name='finish',
        )(py.reshape(ep, n_half // ep, d))

    return jax.shard_map(local, mesh=mesh,
                         in_specs=(tok_spec, tok_spec, tok_spec, P('ep', None, 'tp'), P('ep', None, 'tp'), P('ep', 'tp', None)),
                         out_specs=tok_spec, check_vma=False)
```

profile of v0, /device:TPU:0, one launch (start us, length us, event | category | flops | bytes accessed | tf_op | source)
XLA Modules:
  0.0 338.2 jit_solution(9491365584676773124)
XLA Ops:
  0.0 0.7 convert_element_type.17
  0.7 0.7 pad_maximum_fusion
  1.5 0.7 reshape.112.info
  2.1 33.0 %gather.1 = (bf16[1024,2048]{1,0:T(8,128)(2,1)}, f32[16,8,128]{2,1,0:T(8,128)}) custom-call(bf16[64,2048]{1,0:T(8,128)(2,1)} %x.1, f32[8,128]{1,0:T(8,128)} %reshape.112.info), custom_call_target="tpu_custom_call" | custom-call | tf_op jit(solution)/shard_map/gather/pallas_call | solution.py:442
  35.2 1.0 reshape.113
  36.3 0.2 copy.142
  36.4 0.2 fusion.1
  36.7 0.1 convert_reduce_fusion
  36.9 0.1 select_reduce_fusion.1
  37.2 0.7 dynamic_slice.12
  37.9 0.6 compare_select_fusion
  38.5 1.9 fusion.10
  41.0 0.7 add_add_fusion.meta
  41.8 0.2 convolution_convert_fusion
  42.3 0.8 copy_select_fusion.dest
  43.3 0.2 slice.21
  43.5 0.1 copy.187
  44.2 46.9 %experts.1 = f32[2,4096,2048]{2,1,0:T(8,128)} custom-call(s32[16,8]{1,0:T(8,128)} %add_add_fusion.meta, s32[16,1,1024]{2,1,0:T(1,128)} %copy_select_fusion.dest, bf16[1024,2048]{1,0:T(8,128)(2,1)} %get-tuple-element.204.x, bf16[16,2048,256]{2,1,0:T(8,128)(2,1)} %w1.1, bf16[16,2048,256]{2,1,0:T(8,128)(2,1)} %w3.1, bf16[16,256,2048]{2,1,0:T(8,128)(2,1)} %w2.1), custom_call_target="tpu_custom_call" | custom-call | tf_op jit(solution)/shard_map/experts/pallas_call | solution.py:481
  91.2 212.4 %conditional.1 = (f32[512,2048]{1,0:T(8,128)}) conditional(s32[]{:T(128)} %clamp.3, (s32[1]{0:T(128)}, s32[512,8]{0,1:T(8,128)S(1)}, f32[512,8]{0,1:T(8,128)S(1)}, f32[2,4096,2048]{2,1,0:T(8,128)}) %tuple.50, (s32[1]{0:T(128)}, s32[512,8]{0,1:T(8,128)S(1)}, f32[512,8]{0,1:T(8,128)S(1)}, ...), branch_computations={%region_8.9_spmd, %region_9.10_spmd, %region_10.11_spmd, %region_1... | conditional | bytes 65544 | solution.py:535
  91.2 0.8 copy.164.gates
  92.1 0.8 copy.163.rows
  92.9 210.0 %chain1088.1 = f32[512,2048]{1,0:T(8,128)} custom-call(s32[1]{0:T(128)} %get-tuple-element.157.count, s32[512,8]{1,0:T(8,128)} %copy.163.rows, f32[512,8]{1,0:T(8,128)} %copy.164.gates, f32[2,4096,2048]{2,1,0:T(8,128)} %get-tuple-element.160.src), custom_call_target="tpu_custom_call" | custom-call | tf_op jit(solution)/shard_map/cond/branch_4_fun/chain1088/pallas_call | solution.py:535
  303.6 32.9 %finish.1 = bf16[64,2048]{1,0:T(8,128)(2,1)} custom-call(f32[4,128,2048]{2,1,0:T(8,128)} %bitcast.21), custom_call_target="tpu_custom_call" | custom-call | tf_op jit(solution)/shard_map/finish/pallas_call | solution.py:538
  336.5 1.7 copy.210
  (30 shorter events, 1.7 us)
where the time goes:
time: 344 us; the launch traced here: 338 us
  Pallas kernels  323 us (94%)
  local copies, waits for them, and re-layouts  7.38 us (2%)
  other arithmetic  6.26 us (2%)
    pallas_call x1, Pallas kernels, local(): lax.switch(which, [chain(s, i + 1) for i, s in enumerate(sizes)], total[s...  210 us
    pallas_call x1, Pallas kernels, local(): pl.pallas_call(expert_kernel, grid_spec=pltpu.PrefetchScalarGridSpec(num_...  46.9 us
    pallas_call x1, Pallas kernels, local(): pl.pallas_call(functools.partial(gather_kernel, tp), in_specs=[any_, any_...  33 us
    pallas_call x1, Pallas kernels, local(): pl.pallas_call(functools.partial(finish_kernel, tp), in_specs=[vmem], out...  32.9 us

commit v1 on v0

--- a/solution.py
+++ b/solution.py
@@ -13,11 +13,11 @@
 NS = 8
 NO = NS + 1
 TC = 128
-SIZES = (704, 832, 960, 1024, 1088, 1152, 1216, 1280, 1344, 1408, 1472, 1600, 1792, 2304)
+SIZES = (832, 960, 1024, 1088, 1152, 1216, 1280, 1344, 1408, 1472, 1600, 1792, 2304)
 MESH = pl.DeviceIdType.MESH
 
 
-def expert_kernel(meta, dest, x, w1, w3, w2, out, obuf, carry, cnt, sem):
+def expert_kernel(meta, dest, x, w1, w3, w2, out, obuf, carry, xbuf, cnt, sem):
     e = pl.program_id(0)
     n_tok = x.shape[0]
     n_blk = TM // 8
@@ -31,29 +31,44 @@
             return c
         lax.fori_loop(0, cnt[slot], one, 0)
 
+    def fetch(who, i, s):
+        rows = lax.broadcasted_iota(jnp.int32, (TM, n_tok), 0) + i * TM
+        pick = jnp.where(dest[who] == rows, 1.0, 0.0).astype(jnp.bfloat16)
+        xbuf[s] = jnp.dot(pick, x[...], preferred_element_type=jnp.float32).astype(jnp.bfloat16)
+
+    after = jnp.minimum(e + 1, pl.num_programs(0) - 1)
+
     @pl.when(e == 0)
     def _():
         cnt[0] = 0
         cnt[1] = 0
         cnt[2] = 0
+        cnt[3] = 0
         carry[...] = jnp.zeros_like(carry)
+        fetch(0, 0, 0)
 
     begin = (0, meta[e, 0])
     stop = (meta[e, 0], meta[e, 0] + meta[e, 1])
     place = (meta[e, 2], meta[e, 3])
     short = (meta[e, 4] > 0, meta[e, 5] > 0)
     blocks = stop[1]
+    tiles = (blocks + n_blk - 1) // n_blk
+
+    @pl.when(tiles == 0)
+    def _():
+        fetch(after, 0, cnt[3])
 
     def tile(i, c):
-        rows = lax.broadcasted_iota(jnp.int32, (TM, n_tok), 0) + i * TM
-        pick = jnp.where(dest[0] == rows, 1.0, 0.0).astype(jnp.bfloat16)
-        xs = jnp.dot(pick, x[...], preferred_element_type=jnp.float32).astype(jnp.bfloat16)
+        slot, s = cnt[2], cnt[3]
+        drain(slot)
+        xs = xbuf[s]
         a = jnp.dot(xs, w1[0], preferred_element_type=jnp.float32)
         b = jnp.dot(xs, w3[0], preferred_element_type=jnp.float32)
         h = (jax.nn.silu(a) * b).astype(jnp.bfloat16)
-        slot = cnt[2]
-        drain(slot)
         obuf[slot] = jnp.dot(h, w2[0], preferred_element_type=jnp.float32)
+        more = i + 1 < tiles
+        fetch(jnp.where(more, e, after), jnp.where(more, i + 1, 0), 1 - s)
+        cnt[3] = 1 - s
         low = i * n_blk
         n = jnp.minimum(n_blk, blocks - low)
         kept = jnp.int32(0)
@@ -93,7 +108,7 @@
         cnt[2] = 1 - slot
         return c
 
-    lax.fori_loop(0, (blocks + n_blk - 1) // n_blk, tile, 0)
+    lax.fori_loop(0, tiles, tile, 0)
 
     @pl.when(e == pl.num_programs(0) - 1)
     def _():
@@ -484,7 +499,7 @@
                 num_scalar_prefetch=1,
                 grid=(e_loc,),
                 in_specs=[
-                    pl.BlockSpec((1, 1, n_tok), lambda e, m: (e, 0, 0)),
+                    pl.BlockSpec((e_loc, 1, n_tok), lambda e, m: (0, 0, 0)),
                     pl.BlockSpec((n_tok, d), lambda e, m: (0, 0)),
                     pl.BlockSpec((1, d, f), lambda e, m: (e, 0, 0)),
                     pl.BlockSpec((1, d, f), lambda e, m: (e, 0, 0)),
@@ -494,7 +509,8 @@
                 scratch_shapes=[
                     pltpu.VMEM((2, TM, d), jnp.float32),
                     pltpu.VMEM((2, 8, d), jnp.float32),
-                    pltpu.SMEM((3,), jnp.int32),
+                    pltpu.VMEM((2, TM, d), x.dtype),
+                    pltpu.SMEM((4,), jnp.int32),
                     pltpu.SemaphoreType.DMA((2,)),
                 ]),
             out_shape=jax.ShapeDtypeStruct((2, full, d), jnp.float32),

time: 344 us -> 348 us (1.012)
  Pallas kernels: 323 us -> 329 us
    pallas_call x1, Pallas kernels: 210 us -> 216 us  [local(): lax.switch(which, [chain(s, i + 1) for i, s in enumerate(sizes)], total[s...]
    pallas_call x1, Pallas kernels: 32.9 us -> 28.4 us  [local(): pl.pallas_call(functools.partial(finish_kernel, tp), in_specs=[vmem], out...]
    pallas_call x1, Pallas kernels: 46.9 us -> 51.1 us  [local(): pl.pallas_call(expert_kernel, grid_spec=pltpu.PrefetchScalarGridSpec(num_...]
where the time goes in v1:
time: 348 us; the launch traced here: 344 us
  Pallas kernels  329 us (95%)
  local copies, waits for them, and re-layouts  7.38 us (2%)
  other arithmetic  6.26 us (2%)
    pallas_call x1, Pallas kernels, local(): lax.switch(which, [chain(s, i + 1) for i, s in enumerate(sizes)], total[s...  216 us
    pallas_call x1, Pallas kernels, local(): pl.pallas_call(expert_kernel, grid_spec=pltpu.PrefetchScalarGridSpec(num_...  51.1 us
    pallas_call x1, Pallas kernels, local(): pl.pallas_call(functools.partial(gather_kernel, tp), in_specs=[any_, any_...  33 us
    pallas_call x1, Pallas kernels, local(): pl.pallas_call(functools.partial(finish_kernel, tp), in_specs=[vmem], out...  28.4 us

profile of v1, /device:TPU:0, one launch (start us, length us, event | category | flops | bytes accessed | tf_op | source)
XLA Modules:
  0.0 344.0 jit_solution(9645711724456049593)
XLA Ops:
  0.0 0.7 convert_element_type.17
  0.7 0.7 pad_maximum_fusion
  1.5 0.7 reshape.112.info
  2.1 33.0 %gather.1 = (bf16[1024,2048]{1,0:T(8,128)(2,1)}, f32[16,8,128]{2,1,0:T(8,128)}) custom-call(bf16[64,2048]{1,0:T(8,128)(2,1)} %x.1, f32[8,128]{1,0:T(8,128)} %reshape.112.info), custom_call_target="tpu_custom_call" | custom-call | tf_op jit(solution)/shard_map/gather/pallas_call | solution.py:457
  35.2 1.0 reshape.113
  36.3 0.2 copy.136
  36.4 0.2 fusion.1
  36.7 0.1 convert_reduce_fusion
  36.9 0.1 select_reduce_fusion.1
  37.2 0.7 dynamic_slice.12
  37.9 0.6 compare_select_fusion
  38.5 1.9 fusion.10
  41.0 0.7 add_add_fusion.meta
  41.8 0.2 convolution_convert_fusion
  42.3 0.8 copy_select_fusion.dest
  43.3 0.2 slice.21
  43.5 0.1 copy.179
  44.2 51.1 %experts.1 = f32[2,4096,2048]{2,1,0:T(8,128)} custom-call(s32[16,8]{1,0:T(8,128)} %add_add_fusion.meta, s32[16,1,1024]{2,1,0:T(1,128)} %copy_select_fusion.dest, bf16[1024,2048]{1,0:T(8,128)(2,1)} %get-tuple-element.191.x, bf16[16,2048,256]{2,1,0:T(8,128)(2,1)} %w1.1, bf16[16,2048,256]{2,1,0:T(8,128)(2,1)} %w3.1, bf16[16,256,2048]{2,1,0:T(8,128)(2,1)} %w2.1), custom_call_target="tpu_custom_call" | custom-call | tf_op jit(solution)/shard_map/experts/pallas_call | solution.py:496
  95.3 218.6 %conditional.1 = (f32[512,2048]{1,0:T(8,128)}) conditional(s32[]{:T(128)} %clamp.3, (s32[1]{0:T(128)}, s32[512,8]{0,1:T(8,128)S(1)}, f32[512,8]{0,1:T(8,128)S(1)}, f32[2,4096,2048]{2,1,0:T(8,128)}) %tuple.47, (s32[1]{0:T(128)}, s32[512,8]{0,1:T(8,128)S(1)}, f32[512,8]{0,1:T(8,128)S(1)}, ...), branch_computations={%region_8.9_spmd, %region_9.10_spmd, %region_10.11_spmd, %region_1... | conditional | bytes 65544 | solution.py:551
  95.4 0.8 copy.158.gates
  96.2 0.8 copy.157.rows
  97.0 216.5 %chain1152.1 = f32[512,2048]{1,0:T(8,128)} custom-call(s32[1]{0:T(128)} %get-tuple-element.148.count, s32[512,8]{1,0:T(8,128)} %copy.157.rows, f32[512,8]{1,0:T(8,128)} %copy.158.gates, f32[2,4096,2048]{2,1,0:T(8,128)} %get-tuple-element.151.src), custom_call_target="tpu_custom_call" | custom-call | tf_op jit(solution)/shard_map/cond/branch_4_fun/chain1152/pallas_call | solution.py:551
  313.9 28.4 %finish.1 = bf16[64,2048]{1,0:T(8,128)(2,1)} custom-call(f32[4,128,2048]{2,1,0:T(8,128)} %bitcast.21), custom_call_target="tpu_custom_call" | custom-call | tf_op jit(solution)/shard_map/finish/pallas_call | solution.py:554
  342.4 1.7 copy.201
  (30 shorter events, 1.7 us)
